TPU v7x, 32 devices: a whole 2x2x4 slice. The times are simulated.
32 devices in a mesh: gx: 4 (over y, x), gy: 2 (over core), gz: 4 (over z).
Axes of the slice: x: 2, y: 2, z: 4, core: 2. Of those that a mesh axis runs over, the one named last changes fastest.
Arguments:
- right_side: float32 [81, 16, 16, 512], P(None, 'gx', 'gy', 'gz'), may hold values from -18 to 18
- cell_coef: float32 [16, 16, 128], P('gx', 'gy', 'gz'), may hold values from 0.5 to 2
- cell_matrix: float32 [81, 81], replicated, may hold values from -2 to 16, as said below
- face_coupling: float32 [3, 81, 81], replicated, may hold values from -0.18 to 0.18
- patch_inverse: bfloat16 [648, 648], replicated, may hold values from -0.01 to 0.1, as said below
Outputs:
- solution: float32 [81, 16, 16, 512], P(None, 'gx', 'gy', 'gz')
- residual: float32 [81, 16, 16, 512], P(None, 'gx', 'gy', 'gz')
Inputs may be any that keep to these rules, and one draw needn't show every extreme that they name: `cell_matrix`: symmetric. `patch_inverse`: symmetric.
All inputs are finite; a program needn't handle non-finite values.
Results may differ from a plain program's by a relative error of at most 0.035.
Values may be sent and summed in bfloat16 or wider, within the bound.
A program may use at most 192 MiB of HBM per device.

v0:
```python
import jax
import jax.numpy as jnp
from jax import lax
from jax.sharding import PartitionSpec as P

HIGH = lax.Precision.HIGHEST


def shifted(block, axis, distance):
    devices = range(lax.axis_size(axis))
    route = [((i - distance) % len(devices), i) for i in devices]
    return lax.ppermute(block, axis, route)


def pad_along(values, target, pad_low, pad_high):
    widths = [(0, 0)] * values.ndim
    widths[target] = (pad_low, pad_high)
    return jnp.pad(values, widths)


def cut_along(values, lower_at, upper_at, target):
    return lax.slice_in_dim(values, lower_at, upper_at, axis=target)


def pad_cells(values):
    return jnp.pad(values, ((0, 0), (1, 1), (1, 1), (1, 1), (0, 0)))


def move_x(portion, offset):
    return shifted(portion.astype(jnp.bfloat16), "gx", offset).astype(portion.dtype)


def move_y(portion, offset):
    return shifted(portion.astype(jnp.bfloat16), "gy", offset).astype(portion.dtype)


def move_z(portion, offset):
    return shifted(portion.astype(jnp.bfloat16), "gz", offset).astype(portion.dtype)


def coefficient_frame(cell_coef):
    frame = cell_coef
    arrived = shifted(frame[-1:], "gx", 1)
    frame = jnp.concatenate([arrived, frame], axis=0)
    arrived = shifted(frame[:, -1:], "gy", 1)
    frame = jnp.concatenate([arrived, frame], axis=1)
    arrived = shifted(frame[:, :, -1:], "gz", 1)
    frame = jnp.concatenate([arrived, frame], axis=2)
    return frame


def fetch_lower(scaled, parity):
    region = scaled
    if parity[0] == 0:
        arrived = shifted(region[:, -1:], "gx", 1)
        region = jnp.concatenate([arrived, region[:, :-1]], axis=1)
    if parity[1] == 0:
        arrived = shifted(region[:, :, -1:], "gy", 1)
        region = jnp.concatenate([arrived, region[:, :, :-1]], axis=2)
    if parity[2] == 0:
        arrived = shifted(region[:, :, :, -1:], "gz", 1)
        region = jnp.concatenate([arrived, region[:, :, :, :-1]], axis=3)
    return region


def solve_patches(blocks, region):
    dof_count, extent_x, extent_y, extent_z, rhs_count = region.shape
    blocked = region.reshape(
        dof_count, extent_x // 2, 2, extent_y // 2, 2, extent_z // 2, 2, rhs_count
    )
    solved = jnp.einsum(
        "qijkplmn,pXlYmZnr->qXiYjZkr", blocks, blocked, preferred_element_type=jnp.float32
    )
    return solved.reshape(dof_count, extent_x, extent_y, extent_z, rhs_count)


def fold_changes(correction, parity, coef_frame, cell_matrix, coupling_pairs):
    extent = correction.shape
    coef_region = coef_frame[
        parity[0] : parity[0] + extent[1],
        parity[1] : parity[1] + extent[2],
        parity[2] : parity[2] + extent[3],
    ]
    product = jnp.einsum("pq,qxyzr->pxyzr", cell_matrix, correction, precision=HIGH)
    change = pad_cells(coef_region[None, :, :, :, None] * product)
    for direction in range(3):
        coupled = jnp.einsum(
            "kpq,qxyzr->kpxyzr", coupling_pairs[direction], correction, precision=HIGH
        )
        forward = [(0, 0), (1, 1), (1, 1), (1, 1), (0, 0)]
        backward = list(forward)
        forward[direction + 1] = (0, 2)
        backward[direction + 1] = (2, 0)
        change = change - jnp.pad(coupled[0], forward) - jnp.pad(coupled[1], backward)
    gained = pad_cells(correction)
    senders = (move_x, move_y, move_z)
    for direction in range(3):
        target = direction + 1
        interior = change.shape[target] - 2
        sender = senders[direction]
        if parity[direction] == 0:
            portion = jnp.concatenate(
                [cut_along(change, 0, 2, target), cut_along(gained, 1, 2, target)], axis=target
            )
            arrived = sender(portion, -1)
            change = cut_along(change, 2, interior + 2, target) + pad_along(
                cut_along(arrived, 0, 2, target), target, interior - 2, 0
            )
            gained = cut_along(gained, 2, interior + 2, target) + pad_along(
                cut_along(arrived, 2, 3, target), target, interior - 1, 0
            )
        else:
            from_above = sender(cut_along(change, 0, 1, target), -1)
            from_below = sender(cut_along(change, interior + 1, interior + 2, target), 1)
            change = (
                cut_along(change, 1, interior + 1, target)
                + pad_along(from_above, target, interior - 1, 0)
                + pad_along(from_below, target, 0, interior - 1)
            )
            gained = cut_along(gained, 1, interior + 1, target)
    return (change, gained)


def on_device(right_side, cell_coef, cell_matrix, face_coupling, patch_inverse):
    dof_count = cell_matrix.shape[0]
    extent_x, extent_y, extent_z = cell_coef.shape
    rhs_count = right_side.shape[3] // extent_z
    residual = right_side.reshape(dof_count, extent_x, extent_y, extent_z, rhs_count)
    solution = jnp.zeros_like(residual)
    coef_frame = coefficient_frame(cell_coef)
    scaling_frame = lax.rsqrt(coef_frame)
    scaling_own = scaling_frame[1:, 1:, 1:]
    blocks = patch_inverse.reshape(dof_count, 2, 2, 2, dof_count, 2, 2, 2)
    coupling_pairs = jnp.stack([face_coupling, jnp.swapaxes(face_coupling, 1, 2)], axis=1)
    for colour in range(8):
        parity = (colour // 4, colour // 2 % 2, colour % 2)
        scaled = (scaling_own[None, :, :, :, None] * residual).astype(jnp.bfloat16)
        region = fetch_lower(scaled, parity)
        scaling_region = scaling_frame[
            parity[0] : parity[0] + extent_x,
            parity[1] : parity[1] + extent_y,
            parity[2] : parity[2] + extent_z,
        ]
        correction = scaling_region[None, :, :, :, None] * solve_patches(blocks, region)
        change, gained = fold_changes(correction, parity, coef_frame, cell_matrix, coupling_pairs)
        solution = solution + gained
        residual = residual - change
    return (solution.reshape(right_side.shape), residual.reshape(right_side.shape))


def solution(mesh):
    placed = (P(None, "gx", "gy", "gz"), P("gx", "gy", "gz"), P(), P(), P())
    return jax.shard_map(
        on_device,
        mesh=mesh,
        in_specs=placed,
        out_specs=(P(None, "gx", "gy", "gz"), P(None, "gx", "gy", "gz")),
        check_vma=False,
    )
```

profile of v0, /device:TPU:0, one launch (start us, length us, event | category | flops | bytes accessed | tf_op | source)
XLA Modules:
  0.0 788.8 jit_solution(807500982446739043)
XLA Ops:
  1.3 3.0 collective-permute-start
  18.0 7.5 collective-permute-done.3
  29.6 93.8 %reshape.130 = bf16[81,2,2,2,81,2,2,2]{7,6,5,4,3,2,1,0:T(2,128)(2,1)} reshape(bf16[648,648]{1,0:T(8,128)(2,1)} %param.9) | data formatting | bytes 1679616 | tf_op jit(solution)/shard_map/reshape | solution.py:133
  123.3 109.5 %copy.143 = bf16[81,2,2,2,81,2,2,2,1,1,1]{4,0,7,6,5,3,2,1,10,9,8:T(8,128)(2,1)} copy(bf16[81,2,2,2,81,2,2,2,1,1,1]{7,6,5,4,3,2,1,0,10,9,8:T(2,128)(2,1)} %bitcast.346) | data formatting | bytes 1679616 | tf_op jit(solution)/shard_map/reshape | solution.py:133
  241.1 3.6 fusion.121
  245.1 12.8 %fusion.120 = f32[2,81,4,8,32,4]{1,4,5,3,2,0:T(8,128)S(1)} fusion(f32[2,81,81,1,1,1]{2,1,5,4,3,0:T(8,128)S(1)} %get-tuple-element.112, f32[81,4,8,32,4,1]{0,3,4,2,1,5:T(8,128)S(1)} %bitcast.351), kind=kOutput, calls=%fused_computation.296 | convolution fusion | flops 644972544 | bytes 4033800 | tf_op jit(solution)/shard_map/kpq,qxyzr->kpxyzr/dot_general | solution.py:87
  258.4 3.6 fusion.119
  269.0 24.3 %collective-permute-done.6 = bf16[81,3,10,34,4]{0,4,3,2,1:T(4,128)(2,1)S(1)} collective-permute-done((bf16[81,3,10,34,4]{0,4,3,2,1:T(4,128)(2,1)S(1)}, bf16[81,3,10,34,4]{0,4,3,2,1:T(4,128)(2,1)S(1)}, u32[]{:S(2)}, u32[]{:S(2)}) %collective-permute-start.6) | collective-permute-done | bytes 660992 | tf_op jit(solution)/shard_map/ppermute | solution.py:12
  299.0 3.6 collective-permute-start.8
  302.6 3.1 collective-permute-done.8
  309.1 7.1 collective-permute-done.9
  324.8 3.6 fusion.124
  328.3 3.6 fusion.123
  331.9 3.8 fusion.122
  345.6 24.8 %collective-permute-done.11 = bf16[81,3,10,34,4]{0,4,3,2,1:T(4,128)(2,1)S(1)} collective-permute-done((bf16[81,3,10,34,4]{0,4,3,2,1:T(4,128)(2,1)S(1)}, bf16[81,3,10,34,4]{0,4,3,2,1:T(4,128)(2,1)S(1)}, u32[]{:S(2)}, u32[]{:S(2)}) %collective-permute-start.11) | collective-permute-done | bytes 660992 | tf_op jit(solution)/shard_map/ppermute | solution.py:12
  377.1 3.9 collective-permute-start.13
  383.4 3.7 multiply_convert_fusion.5
  388.5 7.3 collective-permute-done.15
  399.1 3.2 collective-permute-done.16
  405.3 3.6 fusion.127
  408.9 3.6 fusion.126
  412.4 3.8 fusion.125
  426.1 21.8 %collective-permute-done.17 = bf16[81,3,10,34,4]{0,4,3,2,1:T(4,128)(2,1)S(1)} collective-permute-done((bf16[81,3,10,34,4]{0,4,3,2,1:T(4,128)(2,1)S(1)}, bf16[81,3,10,34,4]{0,4,3,2,1:T(4,128)(2,1)S(1)}, u32[]{:S(2)}, u32[]{:S(2)}) %collective-permute-start.17) | collective-permute-done | bytes 660992 | tf_op jit(solution)/shard_map/ppermute | solution.py:12
  453.1 4.6 collective-permute-done.20
  463.0 5.3 collective-permute-done.21
  472.0 3.6 fusion.130
  475.5 3.6 fusion.129
  479.1 4.0 fusion.128
  492.6 22.7 %collective-permute-done.22 = bf16[81,3,10,34,4]{0,4,3,2,1:T(4,128)(2,1)S(1)} collective-permute-done((bf16[81,3,10,34,4]{0,4,3,2,1:T(4,128)(2,1)S(1)}, bf16[81,3,10,34,4]{0,4,3,2,1:T(4,128)(2,1)S(1)}, u32[]{:S(2)}, u32[]{:S(2)}) %collective-permute-start.22) | collective-permute-done | bytes 660992 | tf_op jit(solution)/shard_map/ppermute | solution.py:12
  523.3 2.9 collective-permute-done.26
  531.5 5.1 collective-permute-done.28
  539.5 3.6 fusion.133
  543.0 3.6 fusion.132
  546.6 3.8 fusion.131
  555.5 4.1 fusion.96
  563.8 10.3 %collective-permute-done.30 = bf16[81,1,10,34,4]{0,3,4,2,1:T(8,128)(2,1)S(1)} collective-permute-done((bf16[81,1,10,34,4]{0,3,4,2,1:T(8,128)(2,1)S(1)}, bf16[81,1,10,34,4]{0,3,4,2,1:T(8,128)(2,1)S(1)}, u32[]{:S(2)}, u32[]{:S(2)}) %collective-permute-start.30) | collective-permute-done | bytes 220352 | tf_op jit(solution)/shard_map/ppermute | solution.py:12
  574.1 6.9 collective-permute-done.29
  587.3 4.3 collective-permute-done.32
  596.6 3.6 fusion.136
  600.2 3.6 fusion.135
  603.8 3.8 fusion.134
  612.7 4.1 fusion.95
  621.0 10.3 %collective-permute-done.35 = bf16[81,1,10,34,4]{0,3,4,2,1:T(8,128)(2,1)S(1)} collective-permute-done((bf16[81,1,10,34,4]{0,3,4,2,1:T(8,128)(2,1)S(1)}, bf16[81,1,10,34,4]{0,3,4,2,1:T(8,128)(2,1)S(1)}, u32[]{:S(2)}, u32[]{:S(2)}) %collective-permute-start.35) | collective-permute-done | bytes 220352 | tf_op jit(solution)/shard_map/ppermute | solution.py:12
  631.2 7.3 collective-permute-done.34
  642.5 3.8 collective-permute-start.37
  654.2 4.6 collective-permute-done.39
  663.0 3.6 fusion.139
  666.6 3.6 fusion.138
  670.2 4.0 fusion.137
  680.4 5.2 fusion.92
  689.8 10.3 %collective-permute-done.41 = bf16[81,1,10,34,4]{0,3,4,2,1:T(8,128)(2,1)S(1)} collective-permute-done((bf16[81,1,10,34,4]{0,3,4,2,1:T(8,128)(2,1)S(1)}, bf16[81,1,10,34,4]{0,3,4,2,1:T(8,128)(2,1)S(1)}, u32[]{:S(2)}, u32[]{:S(2)}) %collective-permute-start.41) | collective-permute-done | bytes 220352 | tf_op jit(solution)/shard_map/ppermute | solution.py:12
  700.1 5.2 collective-permute-done.40
  711.9 3.6 collective-permute-done.44
  715.6 3.0 multiply_convert_fusion
  721.1 3.6 fusion.142
  724.6 3.6 fusion.141
  728.2 3.8 fusion.140
  738.1 5.2 fusion.89
  750.4 7.4 collective-permute-done.46
  757.8 6.3 collective-permute-done.45
  769.1 3.6 collective-permute-start.49
  772.7 3.7 fusion.14
  778.9 3.0 copy.140
  781.9 3.5 fusion.16
  (432 shorter events, 216.2 us)
Async XLA Ops:
  0.6 261.9 %copy-start = (f32[81,81]{1,0:T(8,128)S(1)}, f32[81,81]{1,0:T(8,128)}, u32[]{:S(2)}) copy-start(f32[81,81]{1,0:T(8,128)} %param.7) | copy-start | bytes 78736
  1.3 5.5 collective-permute-start
  7.6 1.2 collective-permute-start.1
  8.8 6.1 collective-permute-start.2
  17.0 9.2 %copy-start.39 = (f32[3,81,81]{2,1,0:T(8,128)S(1)}, f32[3,81,81]{2,1,0:T(8,128)}, u32[]{:S(2)}) copy-start(f32[3,81,81]{2,1,0:T(8,128)} %param.8) | copy-start | bytes 236200
  17.0 8.5 %collective-permute-start.3 = (bf16[81,1,8,32,4]{0,3,4,2,1:T(8,128)(2,1)S(1)}, bf16[81,1,8,32,4]{0,3,4,2,1:T(8,128)(2,1)S(1)}, u32[]{:S(2)}, u32[]{:S(2)}) collective-permute-start(bf16[81,1,8,32,4]{0,3,4,2,1:T(8,128)(2,1)S(1)} %slice.913), channel_id=1, source_target_pairs={{24,0},{0,8},{8,16},{16,24},{25,1},{1,9},{9,17},{17,25},{26,2},{2,... | collective-permute-start | bytes 497672 | tf_op jit(solution)/shard_map/ppermute | solution.py:12
  26.2 1.6 collective-permute-start.4
  28.5 207.1 %collective-permute-start.5 = (bf16[81,4,8,1,4]{0,3,4,2,1:T(2,128)(2,1)}, bf16[81,4,8,1,4]{0,3,4,2,1:T(2,128)(2,1)}, u32[]{:S(2)}, u32[]{:S(2)}) collective-permute-start(bf16[81,4,8,1,4]{0,3,4,2,1:T(2,128)(2,1)} %pad_maximum_fusion.25), channel_id=1, source_target_pairs={{3,0},{0,1},{1,2},{2,3},{7,4},{4,5},{5,6},{6,7},{11,8},{8,9},{9,10... | collective-permute-start | bytes 62216 | tf_op jit(solution)/shard_map/ppermute | solution.py:12
  268.3 25.0 %collective-permute-start.6 = (bf16[81,3,10,34,4]{0,4,3,2,1:T(4,128)(2,1)S(1)}, bf16[81,3,10,34,4]{0,4,3,2,1:T(4,128)(2,1)S(1)}, u32[]{:S(2)}, u32[]{:S(2)}) collective-permute-start(bf16[81,3,10,34,4]{0,4,3,2,1:T(4,128)(2,1)S(1)} %copy.94), channel_id=1, source_target_pairs={{8,0},{16,8},{24,16},{0,24},{9,1},{17,9},{25,17},{1,25},{10,2},{18... | collective-permute-start | bytes 1982888 | tf_op jit(solution)/shard_map/ppermute | solution.py:12
  294.8 1.9 collective-permute-start.7
  298.8 8.5 %copy-start.9 = (f32[81,4,8,34,4]{0,3,4,2,1:T(8,128)}, f32[81,4,8,34,4]{0,3,4,2,1:T(8,128)S(1)}, u32[]{:S(2)}) copy-start(f32[81,4,8,34,4]{0,3,4,2,1:T(8,128)S(1)} %slice_add_fusion.15) | copy-start | bytes 4230148
  299.0 6.7 collective-permute-start.8
  307.3 8.8 %collective-permute-start.9 = (bf16[81,1,8,32,4]{0,3,4,2,1:T(8,128)(2,1)S(1)}, bf16[81,1,8,32,4]{0,3,4,2,1:T(8,128)(2,1)S(1)}, u32[]{:S(2)}, u32[]{:S(2)}) collective-permute-start(bf16[81,1,8,32,4]{0,3,4,2,1:T(8,128)(2,1)S(1)} %slice.943), channel_id=1, source_target_pairs={{24,0},{0,8},{8,16},{16,24},{25,1},{1,9},{9,17},{17,25},{26,2},{2,... | collective-permute-start | bytes 497672 | tf_op jit(solution)/shard_map/ppermute | solution.py:12
  317.5 3.3 collective-permute-start.10
  344.9 25.5 %collective-permute-start.11 = (bf16[81,3,10,34,4]{0,4,3,2,1:T(4,128)(2,1)S(1)}, bf16[81,3,10,34,4]{0,4,3,2,1:T(4,128)(2,1)S(1)}, u32[]{:S(2)}, u32[]{:S(2)}) collective-permute-start(bf16[81,3,10,34,4]{0,4,3,2,1:T(4,128)(2,1)S(1)} %copy.102), channel_id=1, source_target_pairs={{8,0},{16,8},{24,16},{0,24},{9,1},{17,9},{25,17},{1,25},{10,2},{18... | collective-permute-start | bytes 1982888 | tf_op jit(solution)/shard_map/ppermute | solution.py:12
  373.2 1.9 collective-permute-start.12
  376.0 7.4 copy-start.10
  376.6 6.8 collective-permute-start.14
  377.1 6.4 collective-permute-start.13
  387.1 8.6 %collective-permute-start.15 = (bf16[81,1,8,32,4]{0,3,4,2,1:T(8,128)(2,1)S(1)}, bf16[81,1,8,32,4]{0,3,4,2,1:T(8,128)(2,1)S(1)}, u32[]{:S(2)}, u32[]{:S(2)}) collective-permute-start(bf16[81,1,8,32,4]{0,3,4,2,1:T(8,128)(2,1)S(1)} %slice.968), channel_id=1, source_target_pairs={{24,0},{0,8},{8,16},{16,24},{25,1},{1,9},{9,17},{17,25},{26,2},{2,... | collective-permute-start | bytes 497672 | tf_op jit(solution)/shard_map/ppermute | solution.py:12
  388.5 14.4 %copy-start.32 = (bf16[81,2,2,2,81,2,2,2,1,1,1]{4,0,7,6,5,3,2,1,10,9,8:T(8,128)(2,1)S(1)}, bf16[81,2,2,2,81,2,2,2,1,1,1]{4,0,7,6,5,3,2,1,10,9,8:T(8,128)(2,1)}, u32[]{:S(2)}) copy-start(bf16[81,2,2,2,81,2,2,2,1,1,1]{4,0,7,6,5,3,2,1,10,9,8:T(8,128)(2,1)} %copy.143) | copy-start | bytes 2519428
  395.8 6.5 collective-permute-start.16
  425.4 22.5 %collective-permute-start.17 = (bf16[81,3,10,34,4]{0,4,3,2,1:T(4,128)(2,1)S(1)}, bf16[81,3,10,34,4]{0,4,3,2,1:T(4,128)(2,1)S(1)}, u32[]{:S(2)}, u32[]{:S(2)}) collective-permute-start(bf16[81,3,10,34,4]{0,4,3,2,1:T(4,128)(2,1)S(1)} %copy.109), channel_id=1, source_target_pairs={{8,0},{16,8},{24,16},{0,24},{9,1},{17,9},{25,17},{1,25},{10,2},{18... | collective-permute-start | bytes 1982888 | tf_op jit(solution)/shard_map/ppermute | solution.py:12
  448.9 1.5 collective-permute-start.19
  449.0 1.6 collective-permute-start.18
  452.2 5.5 collective-permute-start.20
  459.5 8.8 %collective-permute-start.21 = (bf16[81,1,8,32,4]{0,3,4,2,1:T(8,128)(2,1)}, bf16[81,1,8,32,4]{0,3,4,2,1:T(8,128)(2,1)}, u32[]{:S(2)}, u32[]{:S(2)}) collective-permute-start(bf16[81,1,8,32,4]{0,3,4,2,1:T(8,128)(2,1)} %slice.991), channel_id=1, source_target_pairs={{24,0},{0,8},{8,16},{16,24},{25,1},{1,9},{9,17},{17,25},{26,2},{2,... | collective-permute-start | bytes 497672 | tf_op jit(solution)/shard_map/ppermute | solution.py:12
  460.9 7.4 slice-start.2
  491.9 23.4 %collective-permute-start.22 = (bf16[81,3,10,34,4]{0,4,3,2,1:T(4,128)(2,1)S(1)}, bf16[81,3,10,34,4]{0,4,3,2,1:T(4,128)(2,1)S(1)}, u32[]{:S(2)}, u32[]{:S(2)}) collective-permute-start(bf16[81,3,10,34,4]{0,4,3,2,1:T(4,128)(2,1)S(1)} %copy.116), channel_id=1, source_target_pairs={{8,0},{16,8},{24,16},{0,24},{9,1},{17,9},{25,17},{1,25},{10,2},{18... | collective-permute-start | bytes 1982888 | tf_op jit(solution)/shard_map/ppermute | solution.py:12
  517.1 1.5 collective-permute-start.24
  517.2 1.6 collective-permute-start.23
  518.8 7.5 copy-start.12
  519.4 6.8 collective-permute-start.26
  520.7 5.7 collective-permute-start.25
  528.7 1.4 collective-permute-start.27
  528.9 8.1 %copy-start.34 = (bf16[81,2,2,2,81,2,2,2,1,1,1]{4,0,7,6,5,3,2,1,10,9,8:T(8,128)(2,1)S(1)}, bf16[81,2,2,2,81,2,2,2,1,1,1]{4,0,7,6,5,3,2,1,10,9,8:T(8,128)(2,1)}, u32[]{:S(2)}) copy-start(bf16[81,2,2,2,81,2,2,2,1,1,1]{4,0,7,6,5,3,2,1,10,9,8:T(8,128)(2,1)} %copy.143) | copy-start | bytes 2519428
  530.2 6.3 collective-permute-start.28
  560.8 13.3 %collective-permute-start.30 = (bf16[81,1,10,34,4]{0,3,4,2,1:T(8,128)(2,1)S(1)}, bf16[81,1,10,34,4]{0,3,4,2,1:T(8,128)(2,1)S(1)}, u32[]{:S(2)}, u32[]{:S(2)}) collective-permute-start(bf16[81,1,10,34,4]{0,3,4,2,1:T(8,128)(2,1)S(1)} %get-tuple-element.93), channel_id=1, source_target_pairs={{24,0},{0,8},{8,16},{16,24},{25,1},{1,9},{9,17},{17,25},{26,2},{2,... | collective-permute-start | bytes 660968 | tf_op jit(solution)/shard_map/ppermute | solution.py:12
  562.1 18.9 %collective-permute-start.29 = (bf16[81,1,10,34,4]{0,3,4,2,1:T(8,128)(2,1)S(1)}, bf16[81,1,10,34,4]{0,3,4,2,1:T(8,128)(2,1)S(1)}, u32[]{:S(2)}, u32[]{:S(2)}) collective-permute-start(bf16[81,1,10,34,4]{0,3,4,2,1:T(8,128)(2,1)S(1)} %get-tuple-element.92), channel_id=1, source_target_pairs={{8,0},{16,8},{24,16},{0,24},{9,1},{17,9},{25,17},{1,25},{10,2},{18... | collective-permute-start | bytes 660968 | tf_op jit(solution)/shard_map/ppermute | solution.py:12
  581.5 1.9 collective-permute-start.31
  584.0 7.7 copy-start.6
  585.6 6.0 collective-permute-start.32
  592.3 1.4 collective-permute-start.33
  617.9 13.3 %collective-permute-start.35 = (bf16[81,1,10,34,4]{0,3,4,2,1:T(8,128)(2,1)S(1)}, bf16[81,1,10,34,4]{0,3,4,2,1:T(8,128)(2,1)S(1)}, u32[]{:S(2)}, u32[]{:S(2)}) collective-permute-start(bf16[81,1,10,34,4]{0,3,4,2,1:T(8,128)(2,1)S(1)} %get-tuple-element.91), channel_id=1, source_target_pairs={{24,0},{0,8},{8,16},{16,24},{25,1},{1,9},{9,17},{17,25},{26,2},{2,... | collective-permute-start | bytes 660968 | tf_op jit(solution)/shard_map/ppermute | solution.py:12
  618.6 19.9 %collective-permute-start.34 = (bf16[81,1,10,34,4]{0,3,4,2,1:T(8,128)(2,1)S(1)}, bf16[81,1,10,34,4]{0,3,4,2,1:T(8,128)(2,1)S(1)}, u32[]{:S(2)}, u32[]{:S(2)}) collective-permute-start(bf16[81,1,10,34,4]{0,3,4,2,1:T(8,128)(2,1)S(1)} %get-tuple-element.90), channel_id=1, source_target_pairs={{8,0},{16,8},{24,16},{0,24},{9,1},{17,9},{25,17},{1,25},{10,2},{18... | collective-permute-start | bytes 660968 | tf_op jit(solution)/shard_map/ppermute | solution.py:12
  639.1 1.9 collective-permute-start.36
  642.5 6.7 collective-permute-start.38
  642.5 6.6 collective-permute-start.37
  652.5 6.3 collective-permute-start.39
  675.6 30.9 %copy-start.3 = (f32[81,4,8,32,4]{0,3,4,2,1:T(8,128)}, f32[81,4,8,32,4]{0,3,4,2,1:T(8,128)S(1)}, u32[]{:S(2)}) copy-start(f32[81,4,8,32,4]{0,3,4,2,1:T(8,128)S(1)} %broadcast_multiply_fusion.2) | copy-start | bytes 3981316
  686.8 13.3 %collective-permute-start.41 = (bf16[81,1,10,34,4]{0,3,4,2,1:T(8,128)(2,1)S(1)}, bf16[81,1,10,34,4]{0,3,4,2,1:T(8,128)(2,1)S(1)}, u32[]{:S(2)}, u32[]{:S(2)}) collective-permute-start(bf16[81,1,10,34,4]{0,3,4,2,1:T(8,128)(2,1)S(1)} %get-tuple-element.89), channel_id=1, source_target_pairs={{24,0},{0,8},{8,16},{16,24},{25,1},{1,9},{9,17},{17,25},{26,2},{2,... | collective-permute-start | bytes 660968 | tf_op jit(solution)/shard_map/ppermute | solution.py:12
  688.1 17.2 %collective-permute-start.40 = (bf16[81,1,10,34,4]{0,3,4,2,1:T(8,128)(2,1)S(1)}, bf16[81,1,10,34,4]{0,3,4,2,1:T(8,128)(2,1)S(1)}, u32[]{:S(2)}, u32[]{:S(2)}) collective-permute-start(bf16[81,1,10,34,4]{0,3,4,2,1:T(8,128)(2,1)S(1)} %get-tuple-element.88), channel_id=1, source_target_pairs={{8,0},{16,8},{24,16},{0,24},{9,1},{17,9},{25,17},{1,25},{10,2},{18... | collective-permute-start | bytes 660968 | tf_op jit(solution)/shard_map/ppermute | solution.py:12
  706.0 1.5 collective-permute-start.43
  706.0 1.6 collective-permute-start.42
  709.6 5.9 collective-permute-start.44
  738.1 9.4 %copy-start.42 = (bf16[81,4,8,3,4]{0,3,4,2,1:T(4,128)(2,1)S(1)}, bf16[81,4,8,3,4]{0,3,4,2,1:T(4,128)(2,1)}, u32[]{:S(2)}) copy-start(bf16[81,4,8,3,4]{0,3,4,2,1:T(4,128)(2,1)} %copy-done.41) | copy-start | bytes 186628
  744.5 13.3 %collective-permute-start.46 = (bf16[81,1,10,34,4]{0,3,4,2,1:T(8,128)(2,1)S(1)}, bf16[81,1,10,34,4]{0,3,4,2,1:T(8,128)(2,1)S(1)}, u32[]{:S(2)}, u32[]{:S(2)}) collective-permute-start(bf16[81,1,10,34,4]{0,3,4,2,1:T(8,128)(2,1)S(1)} %get-tuple-element.87), channel_id=1, source_target_pairs={{24,0},{0,8},{8,16},{16,24},{25,1},{1,9},{9,17},{17,25},{26,2},{2,... | collective-permute-start | bytes 660968 | tf_op jit(solution)/shard_map/ppermute | solution.py:12
  745.2 18.9 %collective-permute-start.45 = (bf16[81,1,10,34,4]{0,3,4,2,1:T(8,128)(2,1)S(1)}, bf16[81,1,10,34,4]{0,3,4,2,1:T(8,128)(2,1)S(1)}, u32[]{:S(2)}, u32[]{:S(2)}) collective-permute-start(bf16[81,1,10,34,4]{0,3,4,2,1:T(8,128)(2,1)S(1)} %get-tuple-element.86), channel_id=1, source_target_pairs={{8,0},{16,8},{24,16},{0,24},{9,1},{17,9},{25,17},{1,25},{10,2},{18... | collective-permute-start | bytes 660968 | tf_op jit(solution)/shard_map/ppermute | solution.py:12
  764.1 8.5 %copy-start.23 = (f32[81,4,8,34,4]{0,3,4,2,1:T(8,128)S(1)}, f32[81,4,8,34,4]{0,3,4,2,1:T(8,128)}, u32[]{:S(2)}) copy-start(f32[81,4,8,34,4]{0,3,4,2,1:T(8,128)} %copy-done.22) | copy-start | bytes 4230148
  764.7 1.5 collective-permute-start.48
  764.8 1.6 collective-permute-start.47
  765.3 7.4 copy-start.21
  768.5 13.4 %collective-permute-start.50 = (bf16[81,4,8,1,4]{0,3,4,2,1:T(2,128)(2,1)S(1)}, bf16[81,4,8,1,4]{0,3,4,2,1:T(2,128)(2,1)S(1)}, u32[]{:S(2)}, u32[]{:S(2)}) collective-permute-start(bf16[81,4,8,1,4]{0,3,4,2,1:T(2,128)(2,1)S(1)} %get-tuple-element.103), channel_id=1, source_target_pairs={{3,0},{0,1},{1,2},{2,3},{7,4},{4,5},{5,6},{6,7},{11,8},{8,9},{9,10... | collective-permute-start | bytes 62216 | tf_op jit(solution)/shard_map/ppermute | solution.py:12
  769.1 12.9 %collective-permute-start.49 = (bf16[81,4,8,1,4]{0,3,4,2,1:T(2,128)(2,1)S(1)}, bf16[81,4,8,1,4]{0,3,4,2,1:T(2,128)(2,1)S(1)}, u32[]{:S(2)}, u32[]{:S(2)}) collective-permute-start(bf16[81,4,8,1,4]{0,3,4,2,1:T(2,128)(2,1)S(1)} %get-tuple-element.102), channel_id=1, source_target_pairs={{1,0},{2,1},{3,2},{0,3},{5,4},{6,5},{7,6},{4,7},{9,8},{10,9},{11,1... | collective-permute-start | bytes 62216 | tf_op jit(solution)/shard_map/ppermute | solution.py:12
  (52 other events, 134.1 us)
where the time goes:
time: 793 us; the launch traced here: 789 us
  local copies, waits for them, and re-layouts  287 us (36%)
  waiting for transfers between devices  241 us (30%)
  matrix products  122 us (15%)
  other arithmetic  79.1 us (10%)
  starting transfers between devices  57.3 us (7%)
    ppermute x51, waiting for transfers between devices, shifted(): return lax.ppermute(block, axis, route)  241 us
    reshape x2, local copies, waits for them, and re-layouts, on_device(): blocks = patch_inverse.reshape(dof_count, 2, 2, 2, dof_count, 2, 2, 2)  203 us
    dot_general x24, matrix products, fold_changes(): jnp.einsum('kpq,qxyzr->kpxyzr', coupling_pairs[direction], correction, pr...  96.6 us
    ppermute x51, starting transfers between devices, shifted(): return lax.ppermute(block, axis, route)  57.3 us
    another operation x12, other arithmetic  24.2 us
    unnamed x129, local copies, waits for them, and re-layouts  22.4 us
    mul x22, local copies, waits for them, and re-layouts, on_device(): scaling_region[None, :, :, :, None] * solve_patches(blocks, region)  18.1 us
  transfers between devices with their start and end apart: 51, of which 45 were waited for; matrix products, arithmetic and copies ran while one was open for 29% of the time, Pallas kernels for 0%

commit v1 on v0

v1 whole, which is shorter than its diff:
```python
import functools
import jax
import jax.numpy as jnp
from jax import lax
from jax.experimental import pallas as pl
from jax.experimental.pallas import tpu as pltpu
from jax.sharding import PartitionSpec as P

AXES = ("gx", "gy", "gz")
MESH = pl.DeviceIdType.MESH
F32, BF16 = jnp.float32, jnp.bfloat16
LANES = 128


def class_pairs(d):
    bit = 4 >> d
    return [(c, c + bit) for c in range(8) if not c & bit]


def kernel(sizes, dims, start_ref, p_ref, w_ref, sol_ref, res_ref,
           R, S, scaled, corr, ccorr, Xx, Xy, Xz,
           fx, fy, fz, fys, fzs, mxr, mxs, myr, mys, mzr, mzs,
           mxr_s, mxs_s, myr_s, mys_s, mzr_s, mzs_s, send_sem, recv_sem):
    D, Q, nr, ni, njh = dims
    w = 2 * nr
    tiles = [(i, jh) for i in range(ni) for jh in range(njh)]
    C = ni * njh * LANES
    half = njh * LANES
    lane = lax.broadcasted_iota(jnp.int32, (D, LANES), 1)
    jlo0 = (lane // nr) % 2 == 0
    piece = lane // w

    me = [lax.axis_index(a) for a in AXES]

    def neighbour(d, step):
        n = sizes[d]
        return {AXES[d]: lax.rem(me[d] + step + n, n)}

    barrier = pltpu.get_barrier_semaphore()
    for d in range(3):
        for step in (1, -1):
            pl.semaphore_signal(barrier, inc=1, device_id=neighbour(d, step), device_id_type=MESH)

    def rows(c):
        return slice(c * D, (c + 1) * D)

    def cols(i, jh):
        t = i * njh + jh
        return slice(t * LANES, (t + 1) * LANES)

    def get(ref, c):
        return {t: ref[rows(c), cols(*t)].astype(F32) for t in tiles}

    def roll(x, s):
        s = s % LANES
        return pltpu.roll(x, s, 1) if s else x

    for c in range(0, 8, 2):
        ox, oy = c // 4, c // 2 % 2
        for i, jh in tiles:
            a = start_ref[2 * i + ox, 4 * jh + oy]
            b = start_ref[2 * i + ox, 4 * jh + 2 + oy]
            R[rows(c), cols(i, jh)] = jnp.where(jlo0, a, roll(b, nr))
            R[rows(c + 1), cols(i, jh)] = jnp.where(jlo0, roll(a, -nr), b)
    S[...] = jnp.zeros_like(S)
    pl.semaphore_wait(barrier, 6)

    def pack_x(ref, d, last):
        i = ni - 1 if last else 0
        return jnp.concatenate(
            [ref[rows(p[1] if last else p[0]), i * half:(i + 1) * half] for p in class_pairs(0)], 0)

    def pack_y(ref, last):
        out = []
        for p in class_pairs(1):
            c = p[1] if last else p[0]
            jh = njh - 1 if last else 0
            t0 = ref[rows(c), cols(0, jh)].astype(F32)
            t1 = ref[rows(c), cols(1, jh)].astype(F32)
            if last:
                out.append(jnp.where(jlo0, roll(t1, -nr), t0))
            else:
                out.append(jnp.where(jlo0, t0, roll(t1, nr)))
        return jnp.concatenate(out, 0)

    def pack_z(ref, last):
        acc = jnp.zeros((D, LANES), F32)
        n = 0
        for p in class_pairs(2):
            c = p[1] if last else p[0]
            for t in tiles:
                x = ref[rows(c), cols(*t)].astype(F32)
                x = roll(x, w * (n + 1) if last else w * n)
                acc = jnp.where(piece == n, x, acc)
                n += 1
        return acc

    def shifted(d, step, have, halo, pc):
        out = {}
        for i, jh in tiles:
            if d == 0:
                at = i + step
                if 0 <= at < ni:
                    new = have[at, jh]
                else:
                    new = halo(rows(pc), slice(jh * LANES, (jh + 1) * LANES))
            elif d == 1:
                at = jh + step
                if 0 <= at < njh:
                    other = roll(have[i, at], step * nr)
                else:
                    other = halo(rows(pc), slice(0, LANES))
                    if i == 0:
                        other = roll(other, step * nr)
                cur = roll(have[i, jh], -step * nr)
                new = jnp.where(jlo0, cur, other) if step == 1 else jnp.where(jlo0, other, cur)
            else:
                n = pc * len(tiles) + i * njh + jh
                h = halo(slice(0, D), slice(0, LANES))
                if step == 1:
                    new = jnp.where(lane >= LANES - w, roll(h, LANES - w - w * n),
                                    roll(have[i, jh], -w))
                else:
                    new = jnp.where(lane < w, roll(h, -w * n), roll(have[i, jh], w))
            out[i, jh] = new
        return out

    def reader(ref, *at):
        return lambda r, c: ref[(*at, r, c)].astype(F32)

    def remote(src, dst, k, d, step):
        return pltpu.make_async_remote_copy(
            src_ref=src, dst_ref=dst, send_sem=send_sem.at[k], recv_sem=recv_sem.at[k],
            device_id=neighbour(d, step), device_id_type=MESH)

    packers = (lambda ref, last: pack_x(ref, 0, last), pack_y, pack_z)

    def move(d, down, items):
        step = 1 if down else -1
        copies = []
        for ref, staging, landing, at, k in items:
            staging[...] = packers[d](ref, down).astype(staging.dtype)
            copy = remote(staging, landing.at[at], k, d, step)
            copy.start()
            copies.append(copy)
        for (ref, staging, landing, at, k), copy in zip(items, copies):
            copy.wait()
            for pc, (c0, c1) in enumerate(class_pairs(d)):
                old0, old1 = get(ref, c0), get(ref, c1)
                if down:
                    new0, new1 = shifted(d, -1, old1, reader(landing, at), pc), old0
                else:
                    new0, new1 = old1, shifted(d, 1, old0, reader(landing, at), pc)
                for t in tiles:
                    ref[rows(c0), cols(*t)] = new0[t]
                    ref[rows(c1), cols(*t)] = new1[t]

    def pair_rows(q):
        return slice(2 * q * D, 2 * (q + 1) * D)

    def dot(a, b):
        return jnp.dot(a, b, preferred_element_type=F32)

    def colour(t):
        for c in range(8):
            s = R[c * D + Q:c * D + Q + 1, :]
            scaled[rows(c), :] = (s * R[rows(c), :]).astype(BF16)
        for n in range(ni):
            part = slice(n * half, (n + 1) * half)
            solved = dot(p_ref[...], scaled[:, part])
            for c in range(8):
                s = R[c * D + Q:c * D + Q + 1, part]
                k = R[c * D + Q + 1:c * D + Q + 2, part]
                got = s * solved[rows(c), :]
                S[rows(c), part] += got
                corr[rows(c), part] = got.astype(BF16)
                ccorr[rows(c), part] = (k * got).astype(BF16)
        copies = [[None, None] for _ in range(3)]
        for last in (0, 1):
            src = corr.at[4 * D:, half * (ni - 1):] if last else corr.at[:4 * D, :half]
            copies[0][last] = remote(src, fx.at[t, last], t * 6 + last, 0, 1 if last else -1)
            copies[0][last].start()
        for last in (0, 1):
            fys[last] = pack_y(corr, last).astype(BF16)
            copies[1][last] = remote(fys.at[last], fy.at[t, last], t * 6 + 2 + last, 1, 1 if last else -1)
            copies[1][last].start()
        for last in (0, 1):
            fzs[last] = pack_z(corr, last).astype(BF16)
            copies[2][last] = remote(fzs.at[last], fz.at[t, last], t * 6 + 4 + last, 2, 1 if last else -1)
            copies[2][last].start()
        for q in range(4):
            acc = dot(w_ref[0], ccorr[pair_rows(q), :])
            acc += dot(w_ref[1], corr[pair_rows(q), :])
            acc += dot(w_ref[3 if q // 2 == 0 else 4], corr[pair_rows(q ^ 2), :])
            acc += dot(w_ref[5 if q % 2 == 0 else 6], corr[pair_rows(q ^ 1), :])
            R[pair_rows(q), :] -= acc
        for d, X, landing in ((2, Xz, fz), (1, Xy, fy), (0, Xx, fx)):
            for copy in copies[d]:
                copy.wait()
            for pc, (c0, c1) in enumerate(class_pairs(d)):
                new0 = shifted(d, 1, get(corr, c0), reader(landing, t, 0), pc)
                new1 = shifted(d, -1, get(corr, c1), reader(landing, t, 1), pc)
                for at in tiles:
                    X[rows(c0), cols(*at)] = new0[at].astype(BF16)
                    X[rows(c1), cols(*at)] = new1[at].astype(BF16)
        for q in range(4):
            acc = dot(w_ref[2], Xz[pair_rows(q), :])
            acc += dot(w_ref[4 if q // 2 == 0 else 3], Xx[pair_rows(q ^ 2), :])
            acc += dot(w_ref[6 if q % 2 == 0 else 5], Xy[pair_rows(q ^ 1), :])
            R[pair_rows(q), :] -= acc

    def body(u, carry):
        @pl.when(u == 0)
        def _():
            move(0, True, [(R, mxr_s, mxr, 0, 72)])

        @pl.when(u == 2)
        def _():
            move(0, False, [(R, mxr_s, mxr, 1, 73), (S, mxs_s, mxs, 0, 74)])

        @pl.when(lax.rem(u, 2) == 0)
        def _():
            move(1, True, [(R, myr_s, myr, u, 64 + u), (S, mys_s, mys, u, 68 + u)])

        @pl.when(lax.rem(u, 2) == 1)
        def _():
            move(1, False, [(R, myr_s, myr, u, 64 + u), (S, mys_s, mys, u, 68 + u)])

        for v in (0, 1):
            t = 2 * u + v
            move(2, v == 0, [(R, mzr_s, mzr, t, 48 + t), (S, mzs_s, mzs, t, 56 + t)])
            colour(t)
        return carry

    lax.fori_loop(0, 4, body, 0)

    for ref, out in ((S, sol_ref), (R, res_ref)):
        for c in range(0, 8, 2):
            ox, oy = c // 4, c // 2 % 2
            for i, jh in tiles:
                x0 = ref[rows(c), cols(i, jh)]
                x1 = ref[rows(c + 1), cols(i, jh)]
                out[2 * i + ox, 4 * jh + oy] = jnp.where(jlo0, x0, roll(x1, nr))
                out[2 * i + ox, 4 * jh + 2 + oy] = jnp.where(jlo0, roll(x0, -nr), x1)


def on_device(sizes, right_side, cell_coef, cell_matrix, face_coupling, patch_inverse):
    Q = cell_matrix.shape[0]
    X, Y, Z = cell_coef.shape
    lanes = right_side.shape[3]
    nr = lanes // Z
    D = -(-(Q + 2) // 16) * 16
    ni, njh = X // 2, Y // 4
    assert lanes == LANES and ni == 2 and 4 * ni * njh * 2 * nr == LANES
    C = ni * njh * LANES
    coef = jnp.repeat(cell_coef, nr, axis=2)
    extra = jnp.stack([lax.rsqrt(coef), coef], 2)
    start = jnp.concatenate(
        [jnp.transpose(right_side, (1, 2, 0, 3)), extra, jnp.zeros((X, Y, D - Q - 2, lanes), F32)], 2)
    at = jnp.arange(8 * D)
    wanted = jnp.where(at % D < Q, at % D * 8 + at // D, -1)
    pick = (wanted[:, None] == jnp.arange(8 * Q)[None, :]).astype(BF16)
    p = jnp.dot(pick, patch_inverse, preferred_element_type=F32).astype(BF16)
    p = lax.dot_general(p, pick, (((1,), (1,)), ((), ())), preferred_element_type=F32).astype(BF16)

    def padded(m):
        return jnp.pad(m, ((0, D - Q), (0, D - Q)))

    zero = jnp.zeros((D, D), F32)

    def both(a, b, c, d):
        return jnp.concatenate([jnp.concatenate([a, b], 1), jnp.concatenate([c, d], 1)], 0)

    m = padded(cell_matrix)
    f = [-padded(face_coupling[d]) for d in range(3)]
    ft = [x.T for x in f]
    mats = jnp.stack([
        both(m, zero, zero, m),
        both(zero, f[2], ft[2], zero),
        both(zero, ft[2], f[2], zero),
        both(f[0], zero, zero, f[0]),
        both(ft[0], zero, zero, ft[0]),
        both(f[1], zero, zero, f[1]),
        both(ft[1], zero, zero, ft[1]),
    ]).astype(BF16)
    half = njh * LANES
    V = pltpu.VMEM
    scratch = [
        V((8 * D, C), F32), V((8 * D, C), F32), V((8 * D, C), BF16), V((8 * D, C), BF16),
        V((8 * D, C), BF16), V((8 * D, C), BF16), V((8 * D, C), BF16), V((8 * D, C), BF16),
        V((8, 2, 4 * D, half), BF16), V((8, 2, 4 * D, LANES), BF16), V((8, 2, D, LANES), BF16),
        V((2, 4 * D, LANES), BF16), V((2, D, LANES), BF16),
        V((2, 4 * D, half), F32), V((1, 4 * D, half), BF16),
        V((4, 4 * D, LANES), F32), V((4, 4 * D, LANES), BF16),
        V((8, D, LANES), F32), V((8, D, LANES), BF16),
        V((4 * D, half), F32), V((4 * D, half), BF16),
        V((4 * D, LANES), F32), V((4 * D, LANES), BF16),
        V((D, LANES), F32), V((D, LANES), BF16),
        pltpu.SemaphoreType.DMA((75,)), pltpu.SemaphoreType.DMA((75,)),
    ]
    vmem = pl.BlockSpec(memory_space=pltpu.VMEM)
    sol, res = pl.pallas_call(
        functools.partial(kernel, sizes, (D, Q, nr, ni, njh)),
        out_shape=[jax.ShapeDtypeStruct((X, Y, D, lanes), F32)] * 2,
        in_specs=[vmem] * 3,
        out_specs=[vmem] * 2,
        scratch_shapes=scratch,
        compiler_params=pltpu.CompilerParams(
            collective_id=0, has_side_effects=True, vmem_limit_bytes=60 * 1024 * 1024),
    )(start, p, mats)
    return tuple(jnp.transpose(x[:, :, :Q], (2, 0, 1, 3)) for x in (sol, res))


def solution(mesh):
    sizes = tuple(mesh.shape[a] for a in AXES)
    placed = (P(None, "gx", "gy", "gz"), P("gx", "gy", "gz"), P(), P(), P())
    return jax.shard_map(
        functools.partial(on_device, sizes),
        mesh=mesh,
        in_specs=placed,
        out_specs=(P(None, "gx", "gy", "gz"), P(None, "gx", "gy", "gz")),
        check_vma=False,
    )
```

time: 793 us -> 182 us (0.23)
  local copies, waits for them, and re-layouts: 287 us -> 8.98 us
  waiting for transfers between devices: 241 us -> 0 us
  Pallas kernels: 0 us -> 167 us
  matrix products: 122 us -> 3.44 us
  other arithmetic: 79.1 us -> 2.17 us
  starting transfers between devices: 57.3 us -> 0 us
    ppermute x51 -> x0, waiting for transfers between devices: 241 us -> none  [shifted(): return lax.ppermute(block, axis, route)]
    reshape x2, local copies, waits for them, and re-layouts: 203 us -> 0.2 us  [on_device(): coef = jnp.repeat(cell_coef, nr, axis=2)]
    pallas_call x0 -> x1, Pallas kernels: none -> 167 us  [on_device(): pl.pallas_call(functools.partial(kernel, sizes, (D, Q, nr, ni, njh)), out...]
    dot_general x40 -> x1, matrix products: 122 us -> 3.44 us  [on_device(): lax.dot_general(p, pick, (((1,), (1,)), ((), ())), preferred_element_type...]
    ppermute x51 -> x0, starting transfers between devices: 57.3 us -> none  [shifted(): return lax.ppermute(block, axis, route)]
    another operation x12 -> x10, other arithmetic: 24.2 us -> 0.43 us  [the longest x4 0.35 us: on_device(): jnp.stack([both(m, zero, zero, m), both(zero, f[2], ft[2], zero), both(ze...]
    mul x24 -> x0, local copies, waits for them, and re-layouts: 18.5 us -> none  [the longest x22 18.1 us: on_device(): scaling_region[None, :, :, :, None] * solve_patches(blocks, region)]
    unnamed x129 -> x16, local copies, waits for them, and re-layouts: 22.4 us -> 4.52 us
  transfers between devices with their start and end apart: 51 -> 0, of which waited for: 45 -> 0; matrix products, arithmetic and copies ran while one was open for 29% -> 0% of each run, Pallas kernels for 0% -> 0%
where the time goes in v1:
time: 182 us
  Pallas kernels  167 us (92%)
  local copies, waits for them, and re-layouts  8.98 us (5%)
  matrix products  3.44 us (2%)
  other arithmetic  2.17 us (1%)
    pallas_call x1, Pallas kernels, on_device(): pl.pallas_call(functools.partial(kernel, sizes, (D, Q, nr, ni, njh)), out...  167 us
    unnamed x16, local copies, waits for them, and re-layouts  4.52 us

profile of v1, /device:TPU:0, one launch (start us, length us, event | category | flops | bytes accessed | tf_op | source)
XLA Modules:
  0.0 182.2 jit_solution(1241898054154480644)
XLA Ops:
  0.6 0.0 copy-start
  0.7 0.1 pad.62.clone
  0.7 0.9 pad_convert_fusion
  1.6 0.8 copy.31
  2.4 0.8 fusion.49
  3.3 0.1 copy.45
  3.4 0.1 copy.35
  3.5 0.1 copy.46
  3.7 0.1 copy.44
  3.8 0.1 fusion.33
  3.9 0.1 copy.39
  4.0 0.1 fusion.35
  4.1 0.1 copy.40
  4.2 0.1 fusion.37
  4.3 0.1 copy.41
  4.4 0.1 copy.34
  4.5 0.1 copy.32
  4.6 0.1 fusion.22
  4.8 0.1 fusion.25
  4.9 0.1 fusion.28
  5.0 0.1 fusion.31.w_ref
  5.1 0.0 copy-done
  5.1 0.0 copy-start.2
  5.1 0.0 copy-start.1
  5.1 3.4 %fusion.2.p_ref = bf16[768,768]{1,0:T(8,128)(2,1)} fusion(s32[768]{0:T(1024)S(1)} %fusion.45, bf16[648,648]{1,0:T(8,128)(2,1)S(1)} %copy-done), kind=kOutput, calls=%fused_computation.4 | convolution fusion | flops 1411467264 | bytes 2022528 | tf_op jit(solution)/shard_map/dot_general | solution.py:264
  8.6 0.0 copy-done.2
  8.6 0.0 copy-done.1
  8.6 0.8 copy.48
  9.3 1.5 maximum_maximum_fusion.start_ref
  10.8 166.7 %shard_map.68 = (f32[4,8,96,128]{3,2,1,0:T(8,128)}, f32[4,8,96,128]{3,2,1,0:T(8,128)}) custom-call(f32[4,8,96,128]{3,2,1,0:T(8,128)} %maximum_maximum_fusion.start_ref, bf16[768,768]{1,0:T(8,128)(2,1)} %fusion.2.p_ref, bf16[7,192,192]{2,1,0:T(8,128)(2,1)} %copy-done.2), custom_call_target="tpu_custom_call" | custom-call | tf_op jit(solution)/shard_map/pallas_call | solution.py:302
  177.5 2.0 %slice_bitcast_fusion = (f32[81,4,8,128]{3,0,2,1:T(8,128)S(1)}, f32[81,4,8,128]{3,0,2,1:T(8,128)S(1)}) fusion(f32[4,8,96,128]{3,2,1,0:T(8,128)} %get-tuple-element.5, f32[4,8,96,128]{3,2,1,0:T(8,128)} %get-tuple-element.4), kind=kLoop, calls=%fused_computation.7 | loop fusion | bytes 5308416 | tf_op jit(solution)/shard_map/transpose | solution.py:311
  179.5 1.3 copy.43
  180.9 1.3 copy.42
  (13 shorter events, 0.2 us)
Async XLA Ops:
  0.6 4.5 %copy-start = (bf16[648,648]{1,0:T(8,128)(2,1)S(1)}, bf16[648,648]{1,0:T(8,128)(2,1)}, u32[]{:S(2)}) copy-start(bf16[648,648]{1,0:T(8,128)(2,1)} %param.9) | copy-start | bytes 2519428
  5.1 3.5 %copy-start.2 = (bf16[7,192,192]{2,1,0:T(8,128)(2,1)}, bf16[7,192,192]{2,1,0:T(8,128)(2,1)S(1)}, u32[]{:S(2)}) copy-start(bf16[7,192,192]{2,1,0:T(8,128)(2,1)S(1)} %fusion.31.w_ref) | copy-start | bytes 1548292
  5.1 3.5 %copy-start.1 = (f32[81,4,8,128]{3,2,1,0:T(8,128)S(1)}, f32[81,4,8,128]{3,2,1,0:T(8,128)}, u32[]{:S(2)}) copy-start(f32[81,4,8,128]{3,2,1,0:T(8,128)} %param.5) | copy-start | bytes 3981316

commit v2 on v1

v2 whole, which is shorter than its diff:
```python
import functools
import jax
import jax.numpy as jnp
from jax import lax
from jax.experimental import pallas as pl
from jax.experimental.pallas import tpu as pltpu
from jax.sharding import PartitionSpec as P

AXES = ("gx", "gy", "gz")
MESH = pl.DeviceIdType.MESH
F32, BF16 = jnp.float32, jnp.bfloat16
LANES = 128


def class_pairs(d):
    bit = 4 >> d
    return [(c, c + bit) for c in range(8) if not c & bit]


def kernel(sizes, dims, start_ref, p_ref, w_ref, sol_ref, res_ref,
           R, S2, Sx, scaled, corr, ccorr, Xx, Xy, Xz,
           fx, fxe, fy, fz, fxes, fys, fzs, mxr, mxe, mxs, myr, mys, mzr,
           mxr_s, mxs_s, myr_s, mys_s, mzr_s, send_sem, recv_sem):
    D, Q, nr, ni, njh = dims
    w = 2 * nr
    A = Q // 16 * 16
    tiles = [(i, jh) for i in range(ni) for jh in range(njh)]
    C = ni * njh * LANES
    half = njh * LANES
    lane = lax.broadcasted_iota(jnp.int32, (D, LANES), 1)
    jlo0 = (lane // nr) % 2 == 0
    piece = lane // w

    me = [lax.axis_index(a) for a in AXES]

    def neighbour(d, step):
        n = sizes[d]
        return {AXES[d]: lax.rem(me[d] + step + n, n)}

    barrier = pltpu.get_barrier_semaphore()
    for d in range(3):
        for step in (1, -1):
            pl.semaphore_signal(barrier, inc=1, device_id=neighbour(d, step), device_id_type=MESH)

    def rows(c):
        return slice(c * D, (c + 1) * D)

    def cols(i, jh):
        t = i * njh + jh
        return slice(t * LANES, (t + 1) * LANES)

    def get(ref, c):
        return {t: ref[c, :, cols(*t)].astype(F32) for t in tiles}

    def roll(x, s):
        s = s % LANES
        return pltpu.roll(x, s, 1) if s else x

    for c in range(0, 8, 2):
        ox, oy = c // 4, c // 2 % 2
        for i, jh in tiles:
            a = start_ref[2 * i + ox, 4 * jh + oy]
            b = start_ref[2 * i + ox, 4 * jh + 2 + oy]
            R[c, :, cols(i, jh)] = jnp.where(jlo0, a, roll(b, nr))
            R[c + 1, :, cols(i, jh)] = jnp.where(jlo0, roll(a, -nr), b)
    S2[...] = jnp.zeros_like(S2)
    pl.semaphore_wait(barrier, 6)

    def pack_y(ref, last):
        out = []
        for p in class_pairs(1):
            c = p[1] if last else p[0]
            jh = njh - 1 if last else 0
            t0 = ref[c, :, cols(0, jh)].astype(F32)
            t1 = ref[c, :, cols(1, jh)].astype(F32)
            if last:
                out.append(jnp.where(jlo0, roll(t1, -nr), t0))
            else:
                out.append(jnp.where(jlo0, t0, roll(t1, nr)))
        return jnp.stack(out, 0)

    def pack_z(ref, last):
        acc = jnp.zeros((D, LANES), F32)
        n = 0
        for p in class_pairs(2):
            c = p[1] if last else p[0]
            for t in tiles:
                x = ref[c, :, cols(*t)].astype(F32)
                x = roll(x, w * (n + 1) if last else w * n)
                acc = jnp.where(piece == n, x, acc)
                n += 1
        return acc

    def shifted(d, step, have, halo, pc):
        out = {}
        for i, jh in tiles:
            if d == 0:
                at = i + step
                if 0 <= at < ni:
                    new = have[at, jh]
                else:
                    new = halo(slice(jh * LANES, (jh + 1) * LANES))
            elif d == 1:
                at = jh + step
                if 0 <= at < njh:
                    other = roll(have[i, at], step * nr)
                else:
                    other = halo(slice(0, LANES))
                    if i == 0:
                        other = roll(other, step * nr)
                cur = roll(have[i, jh], -step * nr)
                new = jnp.where(jlo0, cur, other) if step == 1 else jnp.where(jlo0, other, cur)
            else:
                n = pc * len(tiles) + i * njh + jh
                h = halo(slice(0, LANES))
                if step == 1:
                    new = jnp.where(lane >= LANES - w, roll(h, LANES - w - w * n),
                                    roll(have[i, jh], -w))
                else:
                    new = jnp.where(lane < w, roll(h, -w * n), roll(have[i, jh], w))
            out[i, jh] = new
        return out

    def read_x(t, last, pc):
        first = lax.broadcasted_iota(jnp.int32, (D - A, LANES), 0) == 0

        def halo(c):
            tail = fxe[t, last, :, c].astype(F32)[pc:pc + 1]
            return jnp.concatenate(
                [fx[t, last, pc, :, c].astype(F32), jnp.where(first, tail, 0.0)], 0)
        return halo

    def read_y(ref, *at):
        return lambda c: ref[(*at, slice(None), c)].astype(F32)

    def remote(src, dst, k, d, step):
        return pltpu.make_async_remote_copy(
            src_ref=src, dst_ref=dst, send_sem=send_sem.at[k], recv_sem=recv_sem.at[k],
            device_id=neighbour(d, step), device_id_type=MESH)

    def move(d, down, copies, halo):
        for copy in copies:
            copy.start()
        for copy in copies:
            copy.wait()
        for pc, (c0, c1) in enumerate(class_pairs(d)):
            old0, old1 = get(R, c0), get(R, c1)
            if down:
                new0, new1 = shifted(d, -1, old1, halo(pc), pc), old0
            else:
                new0, new1 = old1, shifted(d, 1, old0, halo(pc), pc)
            for t in tiles:
                R[c0, :, cols(*t)] = new0[t]
                R[c1, :, cols(*t)] = new1[t]

    def move_x(down, at):
        part = slice((ni - 1) * half, ni * half) if down else slice(0, half)
        cs = slice(4, 8) if down else slice(0, 4)
        mxr_s[...] = R[cs, :A, part].astype(BF16)
        step = 1 if down else -1
        copies = [remote(mxr_s, mxr.at[at], 72 + at, 0, step),
                  remote(R.at[cs, A:A + 8, part], mxe.at[at], 74 + at, 0, step)]
        zeros = jnp.zeros((D - A - 8, LANES), F32)

        def halo(pc):
            return lambda c: jnp.concatenate(
                [mxr[at, pc, :, c].astype(F32), mxe[at, pc, :, c], zeros], 0)
        move(0, down, copies, halo)

    def move_y(down, u):
        myr_s[...] = pack_y(R, down)
        move(1, down, [remote(myr_s, myr.at[u], 64 + u, 1, 1 if down else -1)],
             lambda pc: read_y(myr, u, pc))

    def move_z(down, t):
        mzr_s[...] = pack_z(R, down)
        move(2, down, [remote(mzr_s, mzr.at[t], 48 + t, 2, 1 if down else -1)],
             lambda pc: read_y(mzr, t))

    def sol_y(u):
        return remote(mys_s, mys.at[lax.div(u, 2)], 56 + lax.div(u, 2), 1, -1)

    def sol_x():
        return remote(mxs_s, mxs, 58, 0, -1)

    def pair(ref, q):
        return ref[2 * q:2 * q + 2].reshape(2 * D, C)

    def lessen(q, acc):
        R[2 * q:2 * q + 2] -= acc.reshape(2, D, C)

    def dot(a, b):
        return jnp.dot(a, b, preferred_element_type=F32)

    def colour(t, v, sb):
        for c in range(8):
            s = R[c, Q:Q + 1, :]
            scaled[c] = (s * R[c]).astype(BF16)
        copies = [[None, None] for _ in range(3)]
        extra = [None, None]
        line = lax.broadcasted_iota(jnp.int32, (16, half), 0)
        for n in range(ni):
            part = slice(n * half, (n + 1) * half)
            solved = dot(p_ref[...], scaled[:, :, part].reshape(8 * D, half))
            for c in range(8):
                s = R[c, Q:Q + 1, part]
                k = R[c, Q + 1:Q + 2, part]
                got = s * solved[rows(c), :]
                if v == 1:
                    S2[sb, c, :, part] += got
                corr[c, :, part] = got.astype(BF16)
                ccorr[c, :, part] = (k * got).astype(BF16)
            for last in (0, 1):
                if n != (ni - 1 if last else 0):
                    continue
                step = 1 if last else -1
                tail = jnp.zeros((16, half), F32)
                for pc in range(4):
                    row = corr[4 * last + pc, A:, part].astype(F32)[:1]
                    tail = jnp.where(line == pc, row, tail)
                fxes[last] = tail.astype(BF16)
                copies[0][last] = remote(corr.at[4 * last:4 * last + 4, :A, part], fx.at[t, last],
                                         t * 6 + last, 0, step)
                copies[0][last].start()
                extra[last] = remote(fxes.at[last], fxe.at[t, last], 80 + 2 * t + last, 0, step)
                extra[last].start()
        for last in (0, 1):
            fzs[last] = pack_z(corr, last).astype(BF16)
            copies[2][last] = remote(fzs.at[last], fz.at[t, last], t * 6 + 4 + last, 2, 1 if last else -1)
            copies[2][last].start()
        for last in (0, 1):
            fys[last] = pack_y(corr, last).astype(BF16)
            copies[1][last] = remote(fys.at[last], fy.at[t, last], t * 6 + 2 + last, 1, 1 if last else -1)
            copies[1][last].start()
        for q in range(4):
            acc = dot(w_ref[0], pair(ccorr, q))
            acc += dot(w_ref[1], pair(corr, q))
            acc += dot(w_ref[3 if q // 2 == 0 else 4], pair(corr, q ^ 2))
            acc += dot(w_ref[5 if q % 2 == 0 else 6], pair(corr, q ^ 1))
            lessen(q, acc)

        def fill(d, X, halo0, halo1):
            for pc, (c0, c1) in enumerate(class_pairs(d)):
                new0 = shifted(d, 1, get(corr, c0), halo0(pc), pc)
                new1 = shifted(d, -1, get(corr, c1), halo1(pc), pc)
                for at in tiles:
                    X[c0, :, cols(*at)] = new0[at].astype(BF16)
                    X[c1, :, cols(*at)] = new1[at].astype(BF16)

        for copy in copies[2]:
            copy.wait()
        fill(2, Xz, lambda pc: read_y(fz, t, 0), lambda pc: read_y(fz, t, 1))
        if v == 0:
            for c0, c1 in class_pairs(2):
                S2[sb, c0] += corr[c1].astype(F32)
                S2[sb, c1] += Xz[c0].astype(F32)
        for copy in copies[1]:
            copy.wait()
        fill(1, Xy, lambda pc: read_y(fy, t, 0, pc), lambda pc: read_y(fy, t, 1, pc))
        for q in range(4):
            acc = dot(w_ref[2], pair(Xz, q))
            acc += dot(w_ref[6 if q % 2 == 0 else 5], pair(Xy, q ^ 1))
            lessen(q, acc)
        for copy in copies[0] + extra:
            copy.wait()
        fill(0, Xx, lambda pc: read_x(t, 0, pc), lambda pc: read_x(t, 1, pc))
        for q in range(4):
            lessen(q, dot(w_ref[4 if q // 2 == 0 else 3], pair(Xx, q ^ 2)))

    def body(u, carry):
        @pl.when(u == 0)
        def _():
            move_x(True, 0)

        @pl.when(u == 2)
        def _():
            move_x(False, 1)
            for c in range(8):
                Sx[c] = S2[1, c]
            mxs_s[...] = S2[1, :4, :, :half].astype(BF16)
            sol_x().start()
            S2[1] = jnp.zeros_like(Sx)

        @pl.when(lax.rem(u, 2) == 0)
        def _():
            S2[0] = jnp.zeros_like(Sx)
            move_y(True, u)

        @pl.when(lax.rem(u, 2) == 1)
        def _():
            move_y(False, u)
            mys_s[...] = pack_y(S2.at[0], False).astype(BF16)
            sol_y(u).start()

        for v in (0, 1):
            t = 2 * u + v
            move_z(v == 0, t)
            colour(t, v, lax.rem(u, 2))

        @pl.when(lax.rem(u, 2) == 1)
        def _():
            sol_y(u).wait()
            for pc, (c0, c1) in enumerate(class_pairs(1)):
                S2[1, c0] += S2[0, c1]
                new = shifted(1, 1, get(S2.at[0], c0), read_y(mys, lax.div(u, 2), pc), pc)
                for at in tiles:
                    S2[1, c1, :, cols(*at)] += new[at]
        return carry

    lax.fori_loop(0, 4, body, 0)
    sol_x().wait()
    for pc, (c0, c1) in enumerate(class_pairs(0)):
        S2[1, c0] += Sx[c1]
        new = shifted(0, 1, get(Sx, c0), read_y(mxs, pc), pc)
        for at in tiles:
            S2[1, c1, :, cols(*at)] += new[at]

    for ref, out in ((S2.at[1], sol_ref), (R, res_ref)):
        for c in range(0, 8, 2):
            ox, oy = c // 4, c // 2 % 2
            for i, jh in tiles:
                x0 = ref[c, :, cols(i, jh)]
                x1 = ref[c + 1, :, cols(i, jh)]
                out[2 * i + ox, 4 * jh + oy] = jnp.where(jlo0, x0, roll(x1, nr))
                out[2 * i + ox, 4 * jh + 2 + oy] = jnp.where(jlo0, roll(x0, -nr), x1)


def on_device(sizes, right_side, cell_coef, cell_matrix, face_coupling, patch_inverse):
    Q = cell_matrix.shape[0]
    X, Y, Z = cell_coef.shape
    lanes = right_side.shape[3]
    nr = lanes // Z
    D = -(-(Q + 2) // 16) * 16
    ni, njh = X // 2, Y // 4
    assert lanes == LANES and ni == 2 and 4 * ni * njh * 2 * nr == LANES
    C = ni * njh * LANES
    coef = jnp.repeat(cell_coef, nr, axis=2)
    extra = jnp.stack([lax.rsqrt(coef), coef], 2)
    start = jnp.concatenate(
        [jnp.transpose(right_side, (1, 2, 0, 3)), extra, jnp.zeros((X, Y, D - Q - 2, lanes), F32)], 2)
    at = jnp.arange(8 * D)
    wanted = jnp.where(at % D < Q, at % D * 8 + at // D, -1)
    pick = (wanted[:, None] == jnp.arange(8 * Q)[None, :]).astype(BF16)
    p = jnp.dot(pick, patch_inverse, preferred_element_type=F32).astype(BF16)
    p = lax.dot_general(p, pick, (((1,), (1,)), ((), ())), preferred_element_type=F32).astype(BF16)

    def padded(m):
        return jnp.pad(m, ((0, D - Q), (0, D - Q)))

    zero = jnp.zeros((D, D), F32)

    def both(a, b, c, d):
        return jnp.concatenate([jnp.concatenate([a, b], 1), jnp.concatenate([c, d], 1)], 0)

    m = padded(cell_matrix)
    f = [-padded(face_coupling[d]) for d in range(3)]
    ft = [x.T for x in f]
    mats = jnp.stack([
        both(m, zero, zero, m),
        both(zero, f[2], ft[2], zero),
        both(zero, ft[2], f[2], zero),
        both(f[0], zero, zero, f[0]),
        both(ft[0], zero, zero, ft[0]),
        both(f[1], zero, zero, f[1]),
        both(ft[1], zero, zero, ft[1]),
    ]).astype(BF16)
    half = njh * LANES
    V = pltpu.VMEM
    A = Q // 16 * 16
    assert Q == A + 1
    whole = (8, D, C)
    scratch = [
        V(whole, F32), V((2, *whole), F32), V(whole, F32), V(whole, BF16), V(whole, BF16), V(whole, BF16),
        V(whole, BF16), V(whole, BF16), V(whole, BF16),
        V((8, 2, 4, A, half), BF16), V((8, 2, 16, half), BF16),
        V((8, 2, 4, D, LANES), BF16), V((8, 2, D, LANES), BF16),
        V((2, 16, half), BF16), V((2, 4, D, LANES), BF16), V((2, D, LANES), BF16),
        V((2, 4, A, half), BF16), V((2, 4, 8, half), F32), V((4, D, half), BF16),
        V((4, 4, D, LANES), F32), V((2, 4, D, LANES), BF16), V((8, D, LANES), F32),
        V((4, A, half), BF16), V((4, D, half), BF16),
        V((4, D, LANES), F32), V((4, D, LANES), BF16), V((D, LANES), F32),
        pltpu.SemaphoreType.DMA((96,)), pltpu.SemaphoreType.DMA((96,)),
    ]
    vmem = pl.BlockSpec(memory_space=pltpu.VMEM)
    sol, res = pl.pallas_call(
        functools.partial(kernel, sizes, (D, Q, nr, ni, njh)),
        out_shape=[jax.ShapeDtypeStruct((X, Y, D, lanes), F32)] * 2,
        in_specs=[vmem] * 3,
        out_specs=[vmem] * 2,
        scratch_shapes=scratch,
        compiler_params=pltpu.CompilerParams(
            collective_id=0, has_side_effects=True, vmem_limit_bytes=60 * 1024 * 1024),
    )(start, p, mats)
    return tuple(jnp.transpose(x[:, :, :Q], (2, 0, 1, 3)) for x in (sol, res))


def solution(mesh):
    sizes = tuple(mesh.shape[a] for a in AXES)
    placed = (P(None, "gx", "gy", "gz"), P("gx", "gy", "gz"), P(), P(), P())
    return jax.shard_map(
        functools.partial(on_device, sizes),
        mesh=mesh,
        in_specs=placed,
        out_specs=(P(None, "gx", "gy", "gz"), P(None, "gx", "gy", "gz")),
        check_vma=False,
    )
```

time: 182 us -> 159 us (0.87)
  Pallas kernels: 167 us -> 143 us
    pallas_call x1, Pallas kernels: 167 us -> 143 us  [on_device(): pl.pallas_call(functools.partial(kernel, sizes, (D, Q, nr, ni, njh)), out...]
where the time goes in v2:
time: 159 us
  Pallas kernels  143 us (90%)
  local copies, waits for them, and re-layouts  8.98 us (6%)
  matrix products  3.44 us (2%)
  other arithmetic  2.17 us (1%)
    pallas_call x1, Pallas kernels, on_device(): pl.pallas_call(functools.partial(kernel, sizes, (D, Q, nr, ni, njh)), out...  143 us
    unnamed x16, local copies, waits for them, and re-layouts  4.52 us
    dot_general x1, matrix products, on_device(): lax.dot_general(p, pick, (((1,), (1,)), ((), ())), preferred_element_type...  3.44 us

profile of v2, /device:TPU:0, one launch (start us, length us, event | category | flops | bytes accessed | tf_op | source)
XLA Modules:
  0.0 158.6 jit_solution(13088730989384036291)
XLA Ops:
  0.6 0.0 copy-start
  0.7 0.1 pad.62.clone
  0.7 0.9 pad_convert_fusion
  1.6 0.8 copy.31
  2.4 0.8 fusion.49
  3.3 0.1 copy.45
  3.4 0.1 copy.35
  3.5 0.1 copy.46
  3.7 0.1 copy.44
  3.8 0.1 fusion.33
  3.9 0.1 copy.39
  4.0 0.1 fusion.35
  4.1 0.1 copy.40
  4.2 0.1 fusion.37
  4.3 0.1 copy.41
  4.4 0.1 copy.34
  4.5 0.1 copy.32
  4.6 0.1 fusion.22
  4.8 0.1 fusion.25
  4.9 0.1 fusion.28
  5.0 0.1 fusion.31.w_ref
  5.1 0.0 copy-done
  5.1 0.0 copy-start.2
  5.1 0.0 copy-start.1
  5.1 3.4 %fusion.2.p_ref = bf16[768,768]{1,0:T(8,128)(2,1)} fusion(s32[768]{0:T(1024)S(1)} %fusion.45, bf16[648,648]{1,0:T(8,128)(2,1)S(1)} %copy-done), kind=kOutput, calls=%fused_computation.4 | convolution fusion | flops 1411467264 | bytes 2022528 | tf_op jit(solution)/shard_map/dot_general | solution.py:345
  8.6 0.0 copy-done.2
  8.6 0.0 copy-done.1
  8.6 0.8 copy.48
  9.3 1.5 maximum_maximum_fusion.start_ref
  10.8 143.2 %shard_map.68 = (f32[4,8,96,128]{3,2,1,0:T(8,128)}, f32[4,8,96,128]{3,2,1,0:T(8,128)}) custom-call(f32[4,8,96,128]{3,2,1,0:T(8,128)} %maximum_maximum_fusion.start_ref, bf16[768,768]{1,0:T(8,128)(2,1)} %fusion.2.p_ref, bf16[7,192,192]{2,1,0:T(8,128)(2,1)} %copy-done.2), custom_call_target="tpu_custom_call" | custom-call | tf_op jit(solution)/shard_map/pallas_call | solution.py:385
  154.0 2.0 %slice_bitcast_fusion = (f32[81,4,8,128]{3,0,2,1:T(8,128)S(1)}, f32[81,4,8,128]{3,0,2,1:T(8,128)S(1)}) fusion(f32[4,8,96,128]{3,2,1,0:T(8,128)} %get-tuple-element.5, f32[4,8,96,128]{3,2,1,0:T(8,128)} %get-tuple-element.4), kind=kLoop, calls=%fused_computation.7 | loop fusion | bytes 5308416 | tf_op jit(solution)/shard_map/transpose | solution.py:394
  156.0 1.3 copy.43
  157.3 1.3 copy.42
  (13 shorter events, 0.2 us)
Async XLA Ops:
  0.6 4.5 %copy-start = (bf16[648,648]{1,0:T(8,128)(2,1)S(1)}, bf16[648,648]{1,0:T(8,128)(2,1)}, u32[]{:S(2)}) copy-start(bf16[648,648]{1,0:T(8,128)(2,1)} %param.9) | copy-start | bytes 2519428
  5.1 3.5 %copy-start.2 = (bf16[7,192,192]{2,1,0:T(8,128)(2,1)}, bf16[7,192,192]{2,1,0:T(8,128)(2,1)S(1)}, u32[]{:S(2)}) copy-start(bf16[7,192,192]{2,1,0:T(8,128)(2,1)S(1)} %fusion.31.w_ref) | copy-start | bytes 1548292
  5.1 3.5 %copy-start.1 = (f32[81,4,8,128]{3,2,1,0:T(8,128)S(1)}, f32[81,4,8,128]{3,2,1,0:T(8,128)}, u32[]{:S(2)}) copy-start(f32[81,4,8,128]{3,2,1,0:T(8,128)} %param.5) | copy-start | bytes 3981316

commit v3 on v2

--- a/solution.py
+++ b/solution.py
@@ -17,10 +17,10 @@
     return [(c, c + bit) for c in range(8) if not c & bit]
 
 
-def kernel(sizes, dims, start_ref, p_ref, w_ref, sol_ref, res_ref,
+def kernel(sizes, dims, start_ref, inverse_ref, w_ref, sol_ref, res_ref,
            R, S2, Sx, scaled, corr, ccorr, Xx, Xy, Xz,
            fx, fxe, fy, fz, fxes, fys, fzs, mxr, mxe, mxs, myr, mys, mzr,
-           mxr_s, mxs_s, myr_s, mys_s, mzr_s, send_sem, recv_sem):
+           mxr_s, mxs_s, myr_s, mys_s, mzr_s, p_rows, p_ref, send_sem, recv_sem):
     D, Q, nr, ni, njh = dims
     w = 2 * nr
     A = Q // 16 * 16
@@ -138,9 +138,11 @@
             src_ref=src, dst_ref=dst, send_sem=send_sem.at[k], recv_sem=recv_sem.at[k],
             device_id=neighbour(d, step), device_id_type=MESH)
 
-    def move(d, down, copies, halo):
+    def move(d, down, copies, halo, beside=None):
         for copy in copies:
             copy.start()
+        if beside is not None:
+            beside()
         for copy in copies:
             copy.wait()
         for pc, (c0, c1) in enumerate(class_pairs(d)):
@@ -153,7 +155,7 @@
                 R[c0, :, cols(*t)] = new0[t]
                 R[c1, :, cols(*t)] = new1[t]
 
-    def move_x(down, at):
+    def move_x(down, at, beside=None):
         part = slice((ni - 1) * half, ni * half) if down else slice(0, half)
         cs = slice(4, 8) if down else slice(0, 4)
         mxr_s[...] = R[cs, :A, part].astype(BF16)
@@ -165,7 +167,7 @@
         def halo(pc):
             return lambda c: jnp.concatenate(
                 [mxr[at, pc, :, c].astype(F32), mxe[at, pc, :, c], zeros], 0)
-        move(0, down, copies, halo)
+        move(0, down, copies, halo, beside)
 
     def move_y(down, u):
         myr_s[...] = pack_y(R, down)
@@ -267,10 +269,22 @@
         for q in range(4):
             lessen(q, dot(w_ref[4 if q // 2 == 0 else 3], pair(Xx, q ^ 2)))
 
+    def class_order():
+        r = lax.broadcasted_iota(jnp.int32, (D, 8 * Q), 0)
+        k = lax.broadcasted_iota(jnp.int32, (D, 8 * Q), 1)
+        for c in range(8):
+            pick = jnp.where((k == r * 8 + c) & (r < Q), 1.0, 0.0).astype(BF16)
+            p_rows[c * D:(c + 1) * D, :] = dot(pick, inverse_ref[...]).astype(BF16)
+        k = lax.broadcasted_iota(jnp.int32, (8 * Q, 8 * D), 0)
+        r = lax.broadcasted_iota(jnp.int32, (8 * Q, 8 * D), 1)
+        q = r % D
+        pick = jnp.where((k == q * 8 + r // D) & (q < Q), 1.0, 0.0).astype(BF16)
+        p_ref[...] = dot(p_rows[...], pick).astype(BF16)
+
     def body(u, carry):
         @pl.when(u == 0)
         def _():
-            move_x(True, 0)
+            move_x(True, 0, class_order)
 
         @pl.when(u == 2)
         def _():
@@ -338,12 +352,6 @@
     extra = jnp.stack([lax.rsqrt(coef), coef], 2)
     start = jnp.concatenate(
         [jnp.transpose(right_side, (1, 2, 0, 3)), extra, jnp.zeros((X, Y, D - Q - 2, lanes), F32)], 2)
-    at = jnp.arange(8 * D)
-    wanted = jnp.where(at % D < Q, at % D * 8 + at // D, -1)
-    pick = (wanted[:, None] == jnp.arange(8 * Q)[None, :]).astype(BF16)
-    p = jnp.dot(pick, patch_inverse, preferred_element_type=F32).astype(BF16)
-    p = lax.dot_general(p, pick, (((1,), (1,)), ((), ())), preferred_element_type=F32).astype(BF16)
-
     def padded(m):
         return jnp.pad(m, ((0, D - Q), (0, D - Q)))
 
@@ -379,6 +387,7 @@
         V((4, 4, D, LANES), F32), V((2, 4, D, LANES), BF16), V((8, D, LANES), F32),
         V((4, A, half), BF16), V((4, D, half), BF16),
         V((4, D, LANES), F32), V((4, D, LANES), BF16), V((D, LANES), F32),
+        V((8 * D, 8 * Q), BF16), V((8 * D, 8 * D), BF16),
         pltpu.SemaphoreType.DMA((96,)), pltpu.SemaphoreType.DMA((96,)),
     ]
     vmem = pl.BlockSpec(memory_space=pltpu.VMEM)
@@ -390,7 +399,7 @@
         scratch_shapes=scratch,
         compiler_params=pltpu.CompilerParams(
             collective_id=0, has_side_effects=True, vmem_limit_bytes=60 * 1024 * 1024),
-    )(start, p, mats)
+    )(start, patch_inverse, mats)
     return tuple(jnp.transpose(x[:, :, :Q], (2, 0, 1, 3)) for x in (sol, res))
 
 

time: 159 us -> 155 us (0.975)
  matrix products: 3.44 us -> 0 us
    dot_general x1 -> x0, matrix products: 3.44 us -> none  [on_device(): lax.dot_general(p, pick, (((1,), (1,)), ((), ())), preferred_element_type...]
    unnamed x16 -> x14, local copies, waits for them, and re-layouts: 4.52 us -> 4.51 us
where the time goes in v3:
time: 155 us
  Pallas kernels  143 us (92%)
  local copies, waits for them, and re-layouts  8.9 us (6%)
  other arithmetic  2.16 us (1%)
    pallas_call x1, Pallas kernels, on_device(): pl.pallas_call(functools.partial(kernel, sizes, (D, Q, nr, ni, njh)), out...  143 us
    unnamed x14, local copies, waits for them, and re-layouts  4.51 us

profile of v3, /device:TPU:0, one launch (start us, length us, event | category | flops | bytes accessed | tf_op | source)
XLA Modules:
  0.0 155.0 jit_solution(3108383859639493477)
XLA Ops:
  0.6 0.1 pad.62.clone
  0.7 0.8 pad_convert_fusion
  1.5 0.8 copy.31
  2.3 0.8 fusion.32
  3.2 0.1 copy.45
  3.3 0.1 copy.35
  3.4 0.1 copy.46
  3.6 0.1 copy.44
  3.7 0.0 copy-start
  3.7 0.1 fusion.27
  3.8 0.1 copy.39
  3.9 0.1 fusion.29
  4.0 0.1 copy.40
  4.1 0.1 fusion.31
  4.2 0.1 copy.41
  4.3 0.1 copy.34
  4.4 0.1 copy.32
  4.5 0.1 fusion.16
  4.7 0.1 fusion.19
  4.8 0.1 fusion.22
  4.9 0.1 fusion.25.w_ref
  5.0 0.0 copy-done
  5.0 0.0 copy-start.1
  5.0 0.8 copy.48
  5.8 1.5 maximum_maximum_fusion.start_ref
  7.2 0.0 copy-done.1
  7.3 143.1 %shard_map.68 = (f32[4,8,96,128]{3,2,1,0:T(8,128)}, f32[4,8,96,128]{3,2,1,0:T(8,128)}) custom-call(f32[4,8,96,128]{3,2,1,0:T(8,128)} %maximum_maximum_fusion.start_ref, bf16[648,648]{1,0:T(8,128)(2,1)} %inverse_ref.1, bf16[7,192,192]{2,1,0:T(8,128)(2,1)} %copy-done.1), custom_call_target="tpu_custom_call" | custom-call | tf_op jit(solution)/shard_map/pallas_call | solution.py:394
  150.4 2.0 %slice_bitcast_fusion = (f32[81,4,8,128]{3,0,2,1:T(8,128)S(1)}, f32[81,4,8,128]{3,0,2,1:T(8,128)S(1)}) fusion(f32[4,8,96,128]{3,2,1,0:T(8,128)} %get-tuple-element.5, f32[4,8,96,128]{3,2,1,0:T(8,128)} %get-tuple-element.4), kind=kLoop, calls=%fused_computation.2 | loop fusion | bytes 5308416 | tf_op jit(solution)/shard_map/transpose | solution.py:403
  152.4 1.3 copy.43
  153.7 1.3 copy.42
  (12 shorter events, 0.2 us)
Async XLA Ops:
  3.7 1.3 copy-start
  5.0 2.3 %copy-start.1 = (bf16[7,192,192]{2,1,0:T(8,128)(2,1)}, bf16[7,192,192]{2,1,0:T(8,128)(2,1)S(1)}, u32[]{:S(2)}) copy-start(bf16[7,192,192]{2,1,0:T(8,128)(2,1)S(1)} %fusion.25.w_ref) | copy-start | bytes 1548292
